TPU v7x, 256 devices: a whole 4x4x8 slice. The times are simulated.
256 devices in a mesh: patch: 64 (over y, z, core), sub: 4 (over x).
Axes of the slice: x: 4, y: 4, z: 8, core: 2. Of those that a mesh axis runs over, the one named last changes fastest.
Arguments:
- state: float32 [64, 4, 1, 27, 729], P('patch', 'sub'), may hold values from -6 to 6
- stiff_weight: float32 [64, 96, 9216], P('patch'), may hold values from 0.3 to 3
- volume_weight: float32 [64, 96, 9216], P('patch'), may hold values from 0.5 to 2
- lagrange: float32 [256, 4, 1, 729], P('patch', 'sub'), may hold values from -6 to 6
- mortar: float32 [256, 2, 2, 27, 27], P('patch'), may hold values from -1.25 to 1.25
- links: int32 [256, 6], replicated, may hold values from 0 to 63, as said below
Outputs:
- residual: float32 [64, 4, 1, 27, 729], P('patch', 'sub')
- constraint: float32 [256, 4, 1, 729], P('patch', 'sub')
Inputs may be any that keep to these rules, and one draw needn't show every extreme that they name: `links`: row o * 4 + s is slot s of owner o along patch. Live slots of an owner come first and have both counts in 12 to 27; empty slots are all zero. 2 * 64 slots are live. A live interface joins face 2d + 1 of its first patch to face 2d of its second patch, d being 0 or 1; faces 0 to 3 of every patch lie on exactly one live interface each; the live interfaces of one owner all have the same d. At most 2 faces of one patch lie on live interfaces of one owner; in every draw some owner has 4 live slots and 2 faces of one patch.
All inputs are finite; a program needn't handle non-finite values.
Results may differ from a plain program's by a relative error of at most 0.0001.
Values sent between devices are 32-bit elements; how exact they have to be, the bound alone decides.
A program may use at most 128 MiB of HBM per device.

v0:
```python
import jax
import jax.numpy as jnp
import numpy as np
from jax import lax
from jax.sharding import PartitionSpec as P

ELEMS = 24
DEGREE = 3
FIELDS = 4
stabilize = 0.25
highest = lax.Precision.HIGHEST
gauss_points_four = [
    -0.8611363115940526,
    -0.3399810435848563,
    0.3399810435848563,
    0.8611363115940526,
]
gauss_weights_four = [
    0.3478548451374538,
    0.6521451548625461,
    0.6521451548625461,
    0.3478548451374538,
]


def filled_up(lines, peers):
    spare = -lines.shape[0] % peers
    if not spare:
        return lines
    return jnp.concatenate([lines, jnp.zeros((spare, *lines.shape[1:]), lines.dtype)])


def spread(value, axis, root):
    lines = jnp.where(lax.axis_index(axis) == root, value, jnp.zeros_like(value)).reshape(
        -1, *value.shape[1:][-1:]
    )
    padded = filled_up(lines, lax.axis_size(axis))
    own = lax.psum_scatter(padded, axis, scatter_dimension=0, tiled=True)
    return lax.all_gather(own, axis, axis=0, tiled=True)[: len(lines)].reshape(value.shape)


def in_order(tiles, dim):
    dims = list(tiles.shape[1:])
    dims[dim] *= tiles.shape[0]
    return jnp.moveaxis(tiles, 0, dim).reshape(dims)


def from_everyone(value, axis):
    peers = lax.axis_size(axis)
    return lax.all_to_all(
        jnp.broadcast_to(value[None], (peers, *value.shape)), axis, 0, 0, tiled=True
    )


def gathered_copies(value, axis, dim):
    return in_order(from_everyone(value, axis), dim)


def spline_tables(elements, degree):
    knot_list = np.concatenate(
        [np.zeros(degree), np.arange(elements + 1.0), np.full(degree, float(elements))]
    )
    gauss_nodes = np.array(gauss_points_four)
    gauss_weights = np.array(gauss_weights_four)
    points = (np.arange(elements)[:, None] + (gauss_nodes[None, :] + 1.0) / 2.0).reshape(-1)
    point_weights = np.tile(gauss_weights / 2.0, elements)
    current = np.where(
        (knot_list[None, :-1] <= points[:, None]) & (points[:, None] < knot_list[None, 1:]),
        1.0,
        0.0,
    )
    previous = current
    for order_k in range(1, degree + 1):
        previous = current
        amount = len(knot_list) - 1 - order_k
        current = np.zeros((points.shape[0], amount))
        for column in range(amount):
            left_span = knot_list[column + order_k] - knot_list[column]
            right_span = knot_list[column + order_k + 1] - knot_list[column + 1]
            if left_span > 0:
                current[:, column] += (points - knot_list[column]) / left_span * previous[:, column]
            if right_span > 0:
                current[:, column] += (
                    (knot_list[column + order_k + 1] - points)
                    / right_span
                    * previous[:, column + 1]
                )
    slope_part = np.zeros(current.shape)
    for column in range(current.shape[1]):
        left_span = knot_list[column + degree] - knot_list[column]
        right_span = knot_list[column + degree + 1] - knot_list[column + 1]
        if left_span > 0:
            slope_part[:, column] += degree / left_span * previous[:, column]
        if right_span > 0:
            slope_part[:, column] -= degree / right_span * previous[:, column + 1]
    return (
        jnp.asarray(current, jnp.float32),
        jnp.asarray(slope_part, jnp.float32),
        jnp.asarray(current * point_weights[:, None], jnp.float32),
        jnp.asarray(slope_part * point_weights[:, None], jnp.float32),
    )


def forward(coefficients, outer_matrix, middle_matrix, inner_matrix):
    size_n = outer_matrix.shape[1]
    partial_value = coefficients.reshape(size_n, size_n, size_n)
    partial_value = jnp.einsum("ck,ijk->ijc", inner_matrix, partial_value, precision=highest)
    partial_value = jnp.einsum("bj,ijc->ibc", middle_matrix, partial_value, precision=highest)
    return jnp.dot(
        outer_matrix,
        partial_value.reshape(size_n, -1),
        precision=highest,
        preferred_element_type=jnp.float32,
    )


def backward(values, outer_matrix, middle_matrix, inner_matrix):
    size_n = outer_matrix.shape[1]
    points = outer_matrix.shape[0]
    partial_value = jnp.dot(
        outer_matrix.T, values, precision=highest, preferred_element_type=jnp.float32
    )
    partial_value = partial_value.reshape(size_n, points, points)
    partial_value = jnp.einsum("bj,ibc->ijc", middle_matrix, partial_value, precision=highest)
    partial_value = jnp.einsum("ck,ijc->ijk", inner_matrix, partial_value, precision=highest)
    return partial_value.reshape(size_n, size_n * size_n)


def gradients(coefficients, value_table, slope_table):
    size_n = value_table.shape[1]
    field_cube = coefficients.reshape(size_n, size_n, size_n)
    last_value = jnp.einsum("ck,ijk->ijc", value_table, field_cube, precision=highest)
    last_slope = jnp.einsum("ck,ijk->ijc", slope_table, field_cube, precision=highest)
    mid_plain = jnp.einsum("bj,ijc->ibc", value_table, last_value, precision=highest).reshape(
        size_n, -1
    )
    mid_second = jnp.einsum("bj,ijc->ibc", slope_table, last_value, precision=highest).reshape(
        size_n, -1
    )
    mid_third = jnp.einsum("bj,ijc->ibc", value_table, last_slope, precision=highest).reshape(
        size_n, -1
    )
    return (
        jnp.dot(slope_table, mid_plain, precision=highest, preferred_element_type=jnp.float32),
        jnp.dot(value_table, mid_second, precision=highest, preferred_element_type=jnp.float32),
        jnp.dot(value_table, mid_third, precision=highest, preferred_element_type=jnp.float32),
    )


def backward_sum(fluxes, value_weighted, slope_weighted):
    size_n = value_weighted.shape[1]
    points = value_weighted.shape[0]
    head_first = jnp.dot(slope_weighted.T, fluxes[0], precision=highest).reshape(
        size_n, points, points
    )
    head_second = jnp.dot(value_weighted.T, fluxes[1], precision=highest).reshape(
        size_n, points, points
    )
    head_third = jnp.dot(value_weighted.T, fluxes[2], precision=highest).reshape(
        size_n, points, points
    )
    plain_mid = jnp.einsum("bj,ibc->ijc", value_weighted, head_first, precision=highest)
    plain_mid = plain_mid + jnp.einsum(
        "bj,ibc->ijc", slope_weighted, head_second, precision=highest
    )
    third_mid = jnp.einsum("bj,ibc->ijc", value_weighted, head_third, precision=highest)
    result = jnp.einsum("ck,ijc->ijk", value_weighted, plain_mid, precision=highest)
    result = result + jnp.einsum("ck,ijc->ijk", slope_weighted, third_mid, precision=highest)
    return result.reshape(size_n, size_n * size_n)


def volume_terms(own_field, pressure, stiffness, volume, factor, picker, tables):
    value_table, slope_table, value_weighted, slope_weighted = tables
    partials = gradients(own_field, value_table, slope_table)
    pvalue = forward(pressure, value_table, value_table, value_table)
    fluxes = [factor * stiffness * partials[d] - picker[d] * volume * pvalue for d in range(3)]
    result = backward_sum(fluxes, value_weighted, slope_weighted)
    chosen = picker[0] * partials[0] + picker[1] * partials[1] + picker[2] * partials[2]
    return (result, -backward(volume * chosen, value_weighted, value_weighted, value_weighted))


def per_device(state, stiff_weight, volume_weight, lagrange, mortar, links):
    tables = spline_tables(ELEMS, DEGREE)
    patches = lax.axis_size("patch")
    device = lax.axis_index("patch")
    field_index = lax.axis_index("sub")
    vectors = state.shape[2]
    size_n = state.shape[3]
    slot_count = mortar.shape[0]
    coefficients = state[0, 0]
    stiffness = stiff_weight[0]
    volume = volume_weight[0]
    is_pressure = field_index == FIELDS - 1
    factor = jnp.where(is_pressure, -stabilize, 1.0).astype(jnp.float32)
    picker = (jnp.arange(3) == field_index).astype(jnp.float32)

    def terms_of():

        def one_vector(paired):
            return volume_terms(paired[0], paired[1], stiffness, volume, factor, picker, tables)

        return one_vector

    pressure = spread(coefficients, "sub", FIELDS - 1)
    own_terms, div_terms = lax.map(terms_of(), (coefficients, pressure))
    divergence = lax.psum(div_terms, "sub")
    residual = own_terms + jnp.where(is_pressure, divergence, 0.0)
    field_cube = coefficients.reshape(vectors, size_n, size_n, size_n)
    faces = jnp.stack(
        [field_cube[:, 0], field_cube[:, -1], field_cube[:, :, 0], field_cube[:, :, -1]]
    )
    faces = faces.reshape(4, vectors, size_n * size_n)
    item_count = 2 * slot_count
    item_patch = links[:, 0:2].reshape(patches, item_count)
    item_face = links[:, 2:4].reshape(patches, item_count)
    is_live = jnp.repeat(links[:, 4] > 0, 2).reshape(patches, item_count)
    own_patch = lax.dynamic_index_in_dim(item_patch, device, 0, keepdims=False)
    own_face = lax.dynamic_index_in_dim(item_face, device, 0, keepdims=False)
    own_live = lax.dynamic_index_in_dim(is_live, device, 0, keepdims=False)
    own_rows = lax.dynamic_slice_in_dim(links, device * slot_count, slot_count, 0)
    face_grid = jnp.arange(4)
    gathered = gathered_copies(faces[None], "patch", 0)
    picked = jnp.take(
        gathered.reshape(patches * 4, vectors, size_n * size_n), own_patch * 4 + own_face, axis=0
    )
    picked = picked * own_live.astype(jnp.float32)[:, None, None]
    rank_grid = jnp.arange(size_n)
    row_mask = (rank_grid[None, :] < own_rows[:, 4:5]).astype(jnp.float32)
    col_mask = (rank_grid[None, :] < own_rows[:, 5:6]).astype(jnp.float32)
    left = mortar[:, :, 0] * row_mask[:, None, :, None]
    right = mortar[:, :, 1] * col_mask[:, None, :, None]
    traces_here = picked.reshape(slot_count, 2, vectors, size_n, size_n)
    projected = jnp.einsum("sgai,sgvij,sgbj->sgvab", left, traces_here, right, precision=highest)
    constraint = (projected[:, 0] - projected[:, 1]).reshape(
        slot_count, 1, vectors, size_n * size_n
    )
    multipliers = lagrange[:, 0].reshape(slot_count, vectors, size_n, size_n)
    signs = jnp.array([1.0, -1.0], jnp.float32)
    correction = jnp.einsum("sgai,svab,sgbj->sgvij", left, multipliers, right, precision=highest)
    correction = (correction * signs[None, :, None, None, None]).reshape(
        item_count, vectors, size_n * size_n
    )
    all_blocks = lax.all_gather(correction, "patch", axis=0, tiled=True)
    face_match = (
        (is_live & (item_patch == device)).reshape(-1)[None, :]
        & (item_face.reshape(-1)[None, :] == face_grid[:, None])
    ).astype(jnp.float32)
    face_total = jnp.einsum("ft,tvx->fvx", face_match, all_blocks, precision=highest)
    pieces = face_total.reshape(4, vectors, size_n, size_n)
    result_cube = residual.reshape(vectors, size_n, size_n, size_n)
    result_cube = result_cube.at[:, 0].add(pieces[0])
    result_cube = result_cube.at[:, -1].add(pieces[1])
    result_cube = result_cube.at[:, :, 0].add(pieces[2])
    result_cube = result_cube.at[:, :, -1].add(pieces[3])
    return (result_cube.reshape(1, 1, vectors, size_n, size_n * size_n), constraint)


def solution(mesh):
    return jax.shard_map(
        per_device,
        mesh=mesh,
        in_specs=(
            P("patch", "sub", None, None, None),
            P("patch", None, None),
            P("patch", None, None),
            P("patch", "sub", None, None),
            P("patch", None, None, None, None),
            P(),
        ),
        out_specs=(P("patch", "sub", None, None, None), P("patch", "sub", None, None)),
        check_vma=False,
    )
```

profile of v0, /device:TPU:1, one launch (start us, length us, event | category | flops | bytes accessed | tf_op | source)
XLA Modules:
  0.0 175.8 jit_solution(12599876094862100393)
XLA Ops:
  8.0 0.9 fusion.41
  8.9 10.5 %fusion = f32[8,729]{1,0:T(8,128)S(1)} fusion(f32[28,729]{1,0:T(8,128)S(1)} %concatenate.12), kind=kCustom, calls=%all-reduce-scatter | all-reduce-scatter fusion | flops 23329 | bytes 106000
  19.5 2.8 %collective-permute-start = (f32[3,729]{1,0:T(4,128)S(1)}, f32[3,729]{1,0:T(4,128)S(1)}, u32[]{:S(2)}, u32[]{:S(2)}) collective-permute-start(f32[3,729]{1,0:T(4,128)S(1)} %slice.223), channel_id=1, source_target_pairs={{0,1},{1,2},{2,3},{4,5},{5,6},{6,7},{8,9},{9,10},{10,11},{12,13},{... | collective-permute-start | bytes 26252
  22.3 1.1 reduce.8
  24.4 1.0 broadcast_in_dim.45
  25.3 15.1 %all-to-all-start = ((f32[64,1,4,1,729]{4,2,3,1,0:T(4,128)}), f32[64,1,4,1,729]{4,2,3,1,0:T(4,128)}, u32[]{:S(2)}, u32[]{:S(2)}) async-start(f32[64,1,4,1,729]{4,2,3,1,0:T(4,128)} %broadcast_in_dim.45), calls=%async_computation | async-start | bytes 1572864 | tf_op jit(solution)/shard_map/all_to_all | solution.py:50
  42.2 2.2 %convolution_bitcast_fusion.1 = f32[27,96,96]{1,2,0:T(8,128)S(1)} fusion(f32[27,27,96]{2,1,0:T(8,128)S(1)} %convolution_bitcast_fusion.7, f32[96,27,1]{0,1,2:T(8,128)S(1)} %copy-done.21), kind=kOutput, calls=%fused_computation.38 | convolution fusion | flops 80621568 | bytes 1285632 | tf_op jit(solution)/shard_map/while/body/eval_jaxpr/bj,ijc->ibc/dot_general | solution.py:137
  44.5 2.2 %convolution_bitcast_fusion.3 = f32[27,96,96]{1,2,0:T(8,128)S(1)} fusion(f32[27,27,96]{2,1,0:T(8,128)S(1)} %convolution_bitcast_fusion.7, f32[96,27,1]{0,1,2:T(8,128)S(1)} %copy-done.15), kind=kOutput, calls=%fused_computation.40 | convolution fusion | flops 80621568 | bytes 1285632 | tf_op jit(solution)/shard_map/while/body/eval_jaxpr/bj,ijc->ibc/dot_general | solution.py:134
  47.3 3.3 %convolution_bitcast_fusion = f32[27,96,96]{1,2,0:T(8,128)} fusion(f32[27,27,96]{2,1,0:T(8,128)S(1)} %convolution_bitcast_fusion.6, f32[96,27,1]{0,1,2:T(8,128)S(1)} %copy-done.15), kind=kOutput, calls=%fused_computation.37 | convolution fusion | flops 80621568 | bytes 1285632 | tf_op jit(solution)/shard_map/while/body/eval_jaxpr/bj,ijc->ibc/dot_general | solution.py:140
  50.6 2.8 %copy.46 = f32[27,96,96]{2,1,0:T(8,128)} copy(f32[27,96,96]{1,2,0:T(8,128)} %convolution_bitcast_fusion) | data formatting | bytes 1990656 | tf_op jit(solution)/shard_map/while/body/eval_jaxpr/bj,ijc->ibc/transpose | solution.py:140
  53.5 3.1 %reshape.439 = f32[27,9216]{1,0:T(8,128)} reshape(f32[27,96,96]{2,1,0:T(8,128)} %copy.46) | data formatting | bytes 1990656 | tf_op jit(solution)/shard_map/while/body/eval_jaxpr/reshape | solution.py:140
  56.6 1.5 copy.45
  58.1 3.2 %reshape.437 = f32[27,9216]{1,0:T(8,128)} reshape(f32[27,96,96]{2,1,0:T(8,128)} %copy.45) | data formatting | bytes 1990656 | tf_op jit(solution)/shard_map/while/body/eval_jaxpr/reshape | solution.py:137
  61.8 1.9 %reshape.433 = f32[27,9216]{1,0:T(8,128)} reshape(f32[27,96,96]{2,1,0:T(8,128)S(1)} %copy.42) | data formatting | bytes 1990656 | tf_op jit(solution)/shard_map/while/body/eval_jaxpr/reshape | solution.py:134
  63.6 4.7 %fusion.68 = f32[96,9216]{1,0:T(8,128)S(1)} fusion(f32[96,27]{0,1:T(8,128)S(1)} %copy-done.17, f32[27,9216]{1,0:T(8,128)} %reshape.437), kind=kOutput, calls=%fused_computation.118 | convolution fusion | flops 286654464 | bytes 4544640 | tf_op jit(solution)/shard_map/while/body/eval_jaxpr/dot_general | solution.py:145
  68.3 3.0 %fusion.70 = f32[96,9216]{1,0:T(8,128)S(1)} fusion(f32[96,27]{0,1:T(8,128)S(1)} %copy-done.17, f32[27,9216]{1,0:T(8,128)S(1)} %copy-done.8), kind=kOutput, calls=%fused_computation.120 | convolution fusion | flops 286654464 | bytes 4544640 | tf_op jit(solution)/shard_map/while/body/eval_jaxpr/dot_general | solution.py:146
  71.4 3.0 %fusion.64 = f32[96,9216]{1,0:T(8,128)S(1)} fusion(f32[96,27]{0,1:T(8,128)S(1)} %copy-done.23, f32[27,9216]{1,0:T(8,128)S(1)} %copy-done.9), kind=kOutput, calls=%fused_computation.114 | convolution fusion | flops 286654464 | bytes 4544640 | tf_op jit(solution)/shard_map/while/body/eval_jaxpr/dot_general | solution.py:144
  74.4 1.8 %copy-done.5 = f32[96,9216]{1,0:T(8,128)} copy-done((f32[96,9216]{1,0:T(8,128)}, f32[96,9216]{1,0:T(8,128)S(1)}, u32[]{:S(2)}) %copy-start.5) | copy-done | bytes 3538968
  76.2 4.4 %fusion.13 = f32[27,9216]{1,0:T(8,128)S(1)} fusion(f32[96,27]{0,1:T(8,128)S(1)} %copy-done.18, f32[1,96,9216]{2,1,0:T(8,128)S(1)} %copy-done, f32[96,9216]{1,0:T(8,128)S(1)} %fusion.70, f32[96,9216]{1,0:T(8,128)S(1)} %fusion.68, f32[96,9216]{1,0:T(8,128)S(1)} %fusion.64, f32[]{:T(128)} %bitcast.17, f32[]{:T(128)} %bitcast.12, f32[]{:T(128)} %bitcast.4), kind=kOutput, calls=%fused_computation.14 | convolution fusion | flops 291962880 | bytes 15161484 | tf_op jit(solution)/shard_map/while/body/eval_jaxpr/dot_general | solution.py:120
  81.2 0.9 convolution_bitcast_fusion.4
  82.1 0.7 convolution_negate_fusion
  82.8 0.9 neg.15
  84.6 0.6 copy-done.12
  85.9 0.7 reshape.444
  87.7 0.7 fusion.58
  89.7 0.7 eq.41
  90.7 0.6 reshape.453
  91.5 0.6 and.41
  92.1 0.6 dynamic-slice.33
  93.5 9.1 %all-gather = f32[4,7,729]{2,1,0:T(8,128)S(1)} all-gather(f32[1,7,729]{2,1,0:T(8,128)S(1)} %dynamic-slice_bitcast_fusion), channel_id=1, replica_groups=mesh['patch'=64,'sub'=4] {'sub'}, dimensions={0}, use_global_device_ids=true | all-gather | bytes 102060 | tf_op jit(solution)/shard_map/all_gather | solution.py:39
  103.6 2.2 %convolution_bitcast_fusion.2 = f32[27,96,96]{1,2,0:T(8,128)S(1)} fusion(f32[27,27,96]{2,1,0:T(8,128)S(1)} %fusion.65, f32[96,27,1]{0,1,2:T(8,128)S(1)} %copy-done.15), kind=kOutput, calls=%fused_computation.39 | convolution fusion | flops 80621568 | bytes 1285632 | tf_op jit(solution)/shard_map/while/body/eval_jaxpr/bj,ijc->ibc/dot_general | solution.py:108
  106.3 1.9 %reshape.435 = f32[27,9216]{1,0:T(8,128)} reshape(f32[27,96,96]{2,1,0:T(8,128)S(1)} %copy.44) | data formatting | bytes 1990656 | tf_op jit(solution)/shard_map/while/body/eval_jaxpr/reshape | solution.py:111
  108.2 4.4 %fusion.66 = f32[96,9216]{1,0:T(8,128)S(1)} fusion(f32[96,27]{0,1:T(8,128)} %constant.177.clone, f32[27,9216]{1,0:T(8,128)} %reshape.435), kind=kOutput, calls=%fused_computation.116 | convolution fusion | flops 286654464 | bytes 4544640 | tf_op jit(solution)/shard_map/while/body/eval_jaxpr/dot_general | solution.py:109
  112.7 7.8 %fusion.7 = f32[27,9216]{1,0:T(8,128)} fusion(f32[96,27]{0,1:T(8,128)S(1)} %copy-done.19, f32[96,9216]{1,0:T(8,128)S(1)} %fusion.66, f32[1,96,9216]{2,1,0:T(8,128)S(1)} %copy-done.1, f32[96,9216]{1,0:T(8,128)} %copy-done.4, f32[1,96,9216]{2,1,0:T(8,128)} %param.20, f32[]{:T(128)} %bitcast.12, f32[]{:T(128)S(6)} %select_n.60), kind=kOutput, calls=%fused_computation.10 | convolution fusion | flops 291078144 | bytes 15161480 | tf_op jit(solution)/shard_map/while/body/eval_jaxpr/dot_general | solution.py:156
  120.5 4.1 %fusion.3 = f32[27,9216]{1,0:T(8,128)} fusion(f32[96,27]{0,1:T(8,128)S(1)} %copy-done.22, f32[96,9216]{1,0:T(8,128)S(1)} %fusion.66, f32[1,96,9216]{2,1,0:T(8,128)S(1)} %copy-done.1, f32[96,9216]{1,0:T(8,128)S(1)} %copy-done.6, f32[1,96,9216]{2,1,0:T(8,128)S(1)} %copy-done.2, f32[]{:T(128)} %bitcast.4, f32[]{:T(128)S(6)} %select_n.60), kind=kOutput, calls=%fused_computation.7 | convolution fusion | flops 291078144 | bytes 15161480 | tf_op jit(solution)/shard_map/while/body/eval_jaxpr/dot_general | solution.py:153
  124.6 3.1 %reshape.436 = f32[27,96,96]{2,1,0:T(8,128)} reshape(f32[27,9216]{1,0:T(8,128)} %fusion.3) | data formatting | bytes 1990656 | tf_op jit(solution)/shard_map/while/body/eval_jaxpr/reshape | solution.py:153
  127.7 2.9 %reshape.438 = f32[27,96,96]{2,1,0:T(8,128)} reshape(f32[27,9216]{1,0:T(8,128)} %fusion.7) | data formatting | bytes 1990656 | tf_op jit(solution)/shard_map/while/body/eval_jaxpr/reshape | solution.py:156
  130.6 8.2 %fusion.11 = f32[27,9216]{1,0:T(8,128)} fusion(f32[96,27]{0,1:T(8,128)} %constant.179.clone, f32[96,9216]{1,0:T(8,128)S(1)} %fusion.66, f32[1,96,9216]{2,1,0:T(8,128)} %param.21, f32[96,9216]{1,0:T(8,128)} %copy-done.3, f32[1,96,9216]{2,1,0:T(8,128)} %param.20, f32[]{:T(128)} %bitcast.17, f32[]{:T(128)S(6)} %select_n.60), kind=kOutput, calls=%fused_computation.13 | convolution fusion | flops 291078144 | bytes 15161480 | tf_op jit(solution)/shard_map/while/body/eval_jaxpr/dot_general | solution.py:159
  138.8 1.9 %reshape.440 = f32[27,96,96]{2,1,0:T(8,128)S(1)} reshape(f32[27,9216]{1,0:T(8,128)} %fusion.11) | data formatting | bytes 1990656 | tf_op jit(solution)/shard_map/while/body/eval_jaxpr/reshape | solution.py:159
  140.7 2.2 %fusion.67 = f32[27,96,27]{1,2,0:T(8,128)S(1)} fusion(f32[27,96,96]{2,1,0:T(8,128)} %reshape.436, f32[96,27,1]{0,1,2:T(8,128)S(1)} %copy-done.14), kind=kOutput, calls=%fused_computation.117 | convolution fusion | flops 80621568 | bytes 1285632 | tf_op jit(solution)/shard_map/while/body/eval_jaxpr/bj,ibc->ijc/dot_general | solution.py:162
  142.9 0.9 fusion.33
  144.4 0.9 convolution_bitcast_fusion.5
  146.5 1.4 reshape.454
  147.9 0.7 gather_fusion
  149.5 0.7 sub.32
  150.2 14.0 %all-gather.3.cloned.1.call-done = f32[512,1,729]{2,0,1:T(8,128)} async-done(((f32[8,1,729]{2,0,1:T(8,128)}), f32[512,1,729]{2,0,1:T(8,128)}) %all-gather.3.cloned.1.call-update) | async-done | bytes 1493008 | tf_op jit(solution)/shard_map/all_gather | solution.py:243
  164.3 2.0 %fusion.31 = f32[4,729]{1,0:T(4,128)S(1)} fusion(f32[512,1,729]{2,0,1:T(8,128)} %all-gather.3.cloned.1.call-done, s32[512]{0:T(512)S(1)} %copy-done.26, pred[512]{0:T(512)(128)(4,1)S(1)} %copy-done.28), kind=kOutput, calls=%fused_computation.35 | convolution fusion | flops 17920000 | bytes 1507216 | tf_op jit(solution)/shard_map/ft,tvx->fvx/dot_general | solution.py:248
  167.1 1.0 reshape.450
  (141 shorter events, 13.4 us)
Async XLA Ops:
  8.0 33.2 %copy-start.15 = (f32[96,27,1]{0,1,2:T(8,128)S(1)}, f32[96,27,1]{0,1,2:T(8,128)}, u32[]{:S(2)}) copy-start(f32[96,27,1]{0,1,2:T(8,128)} %constant.193) | copy-start | bytes 31108
  8.0 33.7 %copy-start.21 = (f32[96,27,1]{0,1,2:T(8,128)S(1)}, f32[96,27,1]{0,1,2:T(8,128)}, u32[]{:S(2)}) copy-start(f32[96,27,1]{0,1,2:T(8,128)} %constant.195) | copy-start | bytes 31108
  19.5 73.9 %collective-permute-start = (f32[3,729]{1,0:T(4,128)S(1)}, f32[3,729]{1,0:T(4,128)S(1)}, u32[]{:S(2)}, u32[]{:S(2)}) collective-permute-start(f32[3,729]{1,0:T(4,128)S(1)} %slice.223), channel_id=1, source_target_pairs={{0,1},{1,2},{2,3},{4,5},{5,6},{6,7},{8,9},{9,10},{10,11},{12,13},{... | collective-permute-start | bytes 26252
  25.3 121.1 %all-to-all-start = ((f32[64,1,4,1,729]{4,2,3,1,0:T(4,128)}), f32[64,1,4,1,729]{4,2,3,1,0:T(4,128)}, u32[]{:S(2)}, u32[]{:S(2)}) async-start(f32[64,1,4,1,729]{4,2,3,1,0:T(4,128)} %broadcast_in_dim.45), calls=%async_computation | async-start | bytes 1572864 | tf_op jit(solution)/shard_map/all_to_all | solution.py:50
  40.5 105.5 %all-reduce.5.cloned.1.call-start = ((), (), s32[]{:S(2)}) async-start(), calls=%async_computation.1 | async-start | bytes 196608 | tf_op jit(solution)/shard_map/psum | solution.py:206
  58.1 5.5 %copy-start.17 = (f32[96,27]{0,1:T(8,128)S(1)}, f32[96,27]{0,1:T(8,128)}, u32[]{:S(2)}) copy-start(f32[96,27]{0,1:T(8,128)} %constant.177.clone) | copy-start | bytes 31108
  61.8 6.5 %copy-start.8 = (f32[27,9216]{1,0:T(8,128)S(1)}, f32[27,9216]{1,0:T(8,128)}, u32[]{:S(2)}) copy-start(f32[27,9216]{1,0:T(8,128)} %reshape.439) | copy-start | bytes 2985988
  68.3 6.0 %copy-start.4 = (f32[96,9216]{1,0:T(8,128)}, f32[96,9216]{1,0:T(8,128)S(1)}, u32[]{:S(2)}) copy-start(f32[96,9216]{1,0:T(8,128)S(1)} %fusion.68) | copy-start | bytes 10616836
  68.3 3.0 %copy-start.9 = (f32[27,9216]{1,0:T(8,128)S(1)}, f32[27,9216]{1,0:T(8,128)}, u32[]{:S(2)}) copy-start(f32[27,9216]{1,0:T(8,128)} %reshape.433) | copy-start | bytes 2985988
  68.3 3.0 %copy-start.23 = (f32[96,27]{0,1:T(8,128)S(1)}, f32[96,27]{0,1:T(8,128)}, u32[]{:S(2)}) copy-start(f32[96,27]{0,1:T(8,128)} %constant.178.clone) | copy-start | bytes 31108
  71.3 3.0 %copy-start.3 = (f32[96,9216]{1,0:T(8,128)}, f32[96,9216]{1,0:T(8,128)S(1)}, u32[]{:S(2)}) copy-start(f32[96,9216]{1,0:T(8,128)S(1)} %fusion.70) | copy-start | bytes 10616836
  71.3 4.8 %copy-start = (f32[1,96,9216]{2,1,0:T(8,128)S(1)}, f32[1,96,9216]{2,1,0:T(8,128)}, u32[]{:S(2)}) copy-start(f32[1,96,9216]{2,1,0:T(8,128)} %param.21) | copy-start | bytes 10616836
  71.3 4.8 %copy-start.18 = (f32[96,27]{0,1:T(8,128)S(1)}, f32[96,27]{0,1:T(8,128)}, u32[]{:S(2)}) copy-start(f32[96,27]{0,1:T(8,128)} %constant.179.clone) | copy-start | bytes 31108
  74.3 1.9 %copy-start.5 = (f32[96,9216]{1,0:T(8,128)}, f32[96,9216]{1,0:T(8,128)S(1)}, u32[]{:S(2)}) copy-start(f32[96,9216]{1,0:T(8,128)S(1)} %fusion.64) | copy-start | bytes 10616836
  76.2 5.0 %copy-start.14 = (f32[96,27,1]{0,1,2:T(8,128)S(1)}, f32[96,27,1]{0,1,2:T(8,128)}, u32[]{:S(2)}) copy-start(f32[96,27,1]{0,1,2:T(8,128)} %constant.194) | copy-start | bytes 31108
  80.6 3.1 %copy-start.24 = (s32[256,6]{0,1:T(8,128)S(1)}, s32[256,6]{0,1:T(8,128)}, u32[]{:S(2)}) copy-start(s32[256,6]{0,1:T(8,128)} %param.24) | copy-start | bytes 18436
  80.6 3.3 %copy-start.25 = (f32[4,1,1,729]{3,2,1,0:T(1,128)S(1)}, f32[4,1,1,729]{3,2,1,0:T(1,128)}, u32[]{:S(2)}) copy-start(f32[4,1,1,729]{3,2,1,0:T(1,128)} %param.22) | copy-start | bytes 34996
  80.6 3.5 %copy-start.16 = (f32[4,2,2,27,27]{4,2,3,1,0:T(2,128)S(1)}, f32[4,2,2,27,27]{4,2,3,1,0:T(2,128)}, u32[]{:S(2)}) copy-start(f32[4,2,2,27,27]{4,2,3,1,0:T(2,128)} %param.23) | copy-start | bytes 139972
  80.6 5.0 %copy-start.30 = (f32[2]{0:T(128)S(1)}, f32[2]{0:T(128)}, u32[]{:S(2)}) copy-start(f32[2]{0:T(128)} %constant.181.clone) | copy-start | bytes 28
  81.2 10.9 %copy-start.31 = (u32[256]{0:T(256)S(1)}, u32[256]{0:T(256)}, u32[]{:S(2)}) copy-start(u32[256]{0:T(256)} %constant.191) | copy-start | bytes 3076
  83.6 80.6 %all-gather.3.cloned.1.call-start = ((), (), s32[]{:S(2)}) async-start(), calls=%async_computation.2 | async-start | bytes 1597440 | tf_op jit(solution)/shard_map/all_gather | solution.py:243
  84.6 0.6 copy-start.12
  84.6 1.0 copy-start.10
  108.2 4.4 %copy-start.1 = (f32[1,96,9216]{2,1,0:T(8,128)S(1)}, f32[1,96,9216]{2,1,0:T(8,128)}, u32[]{:S(2)}) copy-start(f32[1,96,9216]{2,1,0:T(8,128)} %param.21) | copy-start | bytes 10616836
  108.2 4.4 %copy-start.19 = (f32[96,27]{0,1:T(8,128)S(1)}, f32[96,27]{0,1:T(8,128)}, u32[]{:S(2)}) copy-start(f32[96,27]{0,1:T(8,128)} %constant.179.clone) | copy-start | bytes 31108
  112.7 7.8 %copy-start.2 = (f32[1,96,9216]{2,1,0:T(8,128)S(1)}, f32[1,96,9216]{2,1,0:T(8,128)}, u32[]{:S(2)}) copy-start(f32[1,96,9216]{2,1,0:T(8,128)} %param.20) | copy-start | bytes 10616836
  112.7 7.8 %copy-start.6 = (f32[96,9216]{1,0:T(8,128)S(1)}, f32[96,9216]{1,0:T(8,128)}, u32[]{:S(2)}) copy-start(f32[96,9216]{1,0:T(8,128)} %copy-done.5) | copy-start | bytes 10616836
  112.7 7.8 %copy-start.22 = (f32[96,27]{0,1:T(8,128)S(1)}, f32[96,27]{0,1:T(8,128)}, u32[]{:S(2)}) copy-start(f32[96,27]{0,1:T(8,128)} %constant.180.clone) | copy-start | bytes 31108
  138.8 4.1 %copy-start.7 = (f32[27,96,96]{2,1,0:T(8,128)S(1)}, f32[27,96,96]{2,1,0:T(8,128)}, u32[]{:S(2)}) copy-start(f32[27,96,96]{2,1,0:T(8,128)} %reshape.438) | copy-start | bytes 2985988
  138.8 4.1 %copy-start.20 = (f32[96,27,1]{0,1,2:T(8,128)S(1)}, f32[96,27,1]{0,1,2:T(8,128)}, u32[]{:S(2)}) copy-start(f32[96,27,1]{0,1,2:T(8,128)} %constant.196) | copy-start | bytes 31108
  143.8 5.0 %copy-start.13 = (f32[4,2,27,27]{3,1,2,0:T(2,128)S(1)}, f32[4,2,27,27]{3,1,2,0:T(2,128)}, u32[]{:S(2)}) copy-start(f32[4,2,27,27]{3,1,2,0:T(2,128)} %copy-done.12) | copy-start | bytes 69988
  143.8 5.0 %copy-start.27 = (f32[4,2]{1,0:T(4,128)S(1)}, f32[4,2]{1,0:T(4,128)}, u32[]{:S(2)}) copy-start(f32[4,2]{1,0:T(4,128)} %reshape.453) | copy-start | bytes 100
  143.8 5.0 %copy-start.29 = (pred[4,2]{1,0:T(4,128)(4,1)S(1)}, pred[4,2]{1,0:T(4,128)(4,1)}, u32[]{:S(2)}) copy-start(pred[4,2]{1,0:T(4,128)(4,1)} %compare_and_fusion.1) | copy-start | bytes 28
  144.3 4.8 %copy-start.11 = (f32[4,2,27,27]{3,1,2,0:T(2,128)S(1)}, f32[4,2,27,27]{3,1,2,0:T(2,128)}, u32[]{:S(2)}) copy-start(f32[4,2,27,27]{3,1,2,0:T(2,128)} %copy-done.10) | copy-start | bytes 69988
  144.3 19.9 %copy-start.26 = (s32[512]{0:T(512)S(1)}, s32[512]{0:T(512)}, u32[]{:S(2)}) copy-start(s32[512]{0:T(512)} %eq.41) | copy-start | bytes 6148
  144.3 19.9 %copy-start.28 = (pred[512]{0:T(512)(128)(4,1)S(1)}, pred[512]{0:T(512)(128)(4,1)}, u32[]{:S(2)}) copy-start(pred[512]{0:T(512)(128)(4,1)} %and.41) | copy-start | bytes 1540
Sparse Core Ops, SparseCore 0:
  83.8 43.7 all-reduce.4
Sparse Core Ops, SparseCore 1:
  87.4 76.8 all-gather.2
where the time goes:
time: 179 us; the launch traced here: 176 us
  matrix products  60.8 us (34%)
  local copies, waits for them, and re-layouts  41.2 us (23%)
  blocking collectives  19.6 us (11%)
  starting transfers between devices  18.2 us (10%)
  between operations  17.3 us (10%)
  waiting for transfers between devices  14.1 us (8%)
  other arithmetic  4.58 us (3%)
    all_to_all x1, starting transfers between devices, from_everyone(): lax.all_to_all(jnp.broadcast_to(value[None], (peers, *value.shape)), axis...  15.1 us
    all_gather x1, waiting for transfers between devices, per_device(): all_blocks = lax.all_gather(correction, 'patch', axis=0, tiled=True)  14 us
    unnamed x1, blocking collectives  10.5 us
    all_gather x1, blocking collectives, spread(): lax.all_gather(own, axis, axis=0, tiled=True)[:len(lines)]  9.12 us
    dot_general x1, matrix products, backward_sum(): jnp.dot(value_weighted.T, fluxes[2], precision=highest)  8.23 us
    dot_general x1, matrix products, backward_sum(): jnp.dot(value_weighted.T, fluxes[1], precision=highest)  7.78 us
    dot_general x1, matrix products, gradients(): jnp.dot(value_table, mid_second, precision=highest, preferred_element_typ...  4.66 us
    dot_general x1, matrix products, backward(): jnp.dot(outer_matrix.T, values, precision=highest, preferred_element_type...  4.4 us
  transfers between devices with their start and end apart: 4, of which 1 were waited for; matrix products, arithmetic and copies ran while one was open for 57% of the time, Pallas kernels for 0%

commit v1 on v0

--- a/solution.py
+++ b/solution.py
@@ -21,6 +21,13 @@
     0.6521451548625461,
     0.3478548451374538,
 ]
+
+
+def all_by_exchange(x, axis, dim):
+    size = lax.axis_size(axis)
+    tiles = jnp.stack([x for _ in range(size)])
+    tiles = lax.all_to_all(tiles, axis, split_axis=0, concat_axis=0)
+    return jnp.concatenate(tiles, axis=dim)
 
 
 def filled_up(lines, peers):
@@ -240,7 +247,7 @@
     correction = (correction * signs[None, :, None, None, None]).reshape(
         item_count, vectors, size_n * size_n
     )
-    all_blocks = lax.all_gather(correction, "patch", axis=0, tiled=True)
+    all_blocks = all_by_exchange(correction, "patch", 0)
     face_match = (
         (is_live & (item_patch == device)).reshape(-1)[None, :]
         & (item_face.reshape(-1)[None, :] == face_grid[:, None])

time: 179 us -> 188 us (1.050)
  starting transfers between devices: 18.2 us -> 31.3 us
  waiting for transfers between devices: 14.1 us -> 5.97 us
  matrix products: 60.8 us -> 64.4 us
    all_gather x1 -> x0, waiting for transfers between devices: 14 us -> none  [per_device(): all_blocks = lax.all_gather(correction, 'patch', axis=0, tiled=True)]
    all_to_all x0 -> x1, starting transfers between devices: none -> 13.2 us  [all_by_exchange(): tiles = lax.all_to_all(tiles, axis, split_axis=0, concat_axis=0)]
    all_to_all x0 -> x1, waiting for transfers between devices: none -> 5.94 us  [all_by_exchange(): tiles = lax.all_to_all(tiles, axis, split_axis=0, concat_axis=0)]
    dot_general x1, matrix products: 4.1 us -> 8.25 us  [backward_sum(): jnp.dot(slope_weighted.T, fluxes[0], precision=highest)]
    another operation x5 -> x7, local copies, waits for them, and re-layouts: 0.5 us -> 3.25 us  [the longest x2 2.75 us: all_by_exchange(): tiles = jnp.stack([x for _ in range(size)])]
where the time goes in v1:
time: 188 us; the launch traced here: 185 us
  matrix products  64.4 us (34%)
  local copies, waits for them, and re-layouts  42.5 us (23%)
  starting transfers between devices  31.3 us (17%)
  blocking collectives  20.1 us (11%)
  between operations  15.7 us (8%)
  waiting for transfers between devices  5.97 us (3%)
  other arithmetic  4.6 us (2%)
    all_to_all x1, starting transfers between devices, from_everyone(): lax.all_to_all(jnp.broadcast_to(value[None], (peers, *value.shape)), axis...  15.1 us
    all_to_all x1, starting transfers between devices, all_by_exchange(): tiles = lax.all_to_all(tiles, axis, split_axis=0, concat_axis=0)  13.2 us
    unnamed x1, blocking collectives  10.5 us
    all_gather x1, blocking collectives, spread(): lax.all_gather(own, axis, axis=0, tiled=True)[:len(lines)]  9.56 us
    dot_general x1, matrix products, backward_sum(): jnp.dot(slope_weighted.T, fluxes[0], precision=highest)  8.25 us
    dot_general x1, matrix products, backward_sum(): jnp.dot(value_weighted.T, fluxes[2], precision=highest)  8.16 us
    dot_general x1, matrix products, backward_sum(): jnp.dot(value_weighted.T, fluxes[1], precision=highest)  7.22 us
    all_to_all x1, waiting for transfers between devices, all_by_exchange(): tiles = lax.all_to_all(tiles, axis, split_axis=0, concat_axis=0)  5.94 us
  transfers between devices with their start and end apart: 4, of which 1 were waited for; matrix products, arithmetic and copies ran while one was open for 57% of the time, Pallas kernels for 0%

profile of v1, /device:TPU:1, one launch (start us, length us, event | category | flops | bytes accessed | tf_op | source)
XLA Modules:
  0.0 184.5 jit_solution(6810072813569362978)
XLA Ops:
  7.2 0.9 fusion.41
  8.1 10.5 %fusion = f32[8,729]{1,0:T(8,128)S(1)} fusion(f32[28,729]{1,0:T(8,128)S(1)} %concatenate.12), kind=kCustom, calls=%all-reduce-scatter | all-reduce-scatter fusion | flops 23329 | bytes 106000
  18.7 2.8 %collective-permute-start = (f32[3,729]{1,0:T(4,128)S(1)}, f32[3,729]{1,0:T(4,128)S(1)}, u32[]{:S(2)}, u32[]{:S(2)}) collective-permute-start(f32[3,729]{1,0:T(4,128)S(1)} %slice.223), channel_id=1, source_target_pairs={{0,1},{1,2},{2,3},{4,5},{5,6},{6,7},{8,9},{9,10},{10,11},{12,13},{... | collective-permute-start | bytes 26252
  21.4 1.1 reduce.8
  23.5 1.0 broadcast_in_dim.45
  24.5 15.1 %all-to-all-start.1 = ((f32[64,1,4,1,729]{4,2,3,1,0:T(4,128)}), f32[64,1,4,1,729]{4,2,3,1,0:T(4,128)}, u32[]{:S(2)}, u32[]{:S(2)}) async-start(f32[64,1,4,1,729]{4,2,3,1,0:T(4,128)} %broadcast_in_dim.45), calls=%async_computation.1 | async-start | bytes 1572864 | tf_op jit(solution)/shard_map/all_to_all | solution.py:57
  41.4 2.2 %convolution_bitcast_fusion.1 = f32[27,96,96]{1,2,0:T(8,128)S(1)} fusion(f32[27,27,96]{2,1,0:T(8,128)S(1)} %convolution_bitcast_fusion.7, f32[96,27,1]{0,1,2:T(8,128)S(1)} %copy-done.19), kind=kOutput, calls=%fused_computation.38 | convolution fusion | flops 80621568 | bytes 1285632 | tf_op jit(solution)/shard_map/while/body/eval_jaxpr/bj,ijc->ibc/dot_general | solution.py:144
  43.6 2.2 %convolution_bitcast_fusion.3 = f32[27,96,96]{1,2,0:T(8,128)S(1)} fusion(f32[27,27,96]{2,1,0:T(8,128)S(1)} %convolution_bitcast_fusion.7, f32[96,27,1]{0,1,2:T(8,128)S(1)} %copy-done.13), kind=kOutput, calls=%fused_computation.40 | convolution fusion | flops 80621568 | bytes 1285632 | tf_op jit(solution)/shard_map/while/body/eval_jaxpr/bj,ijc->ibc/dot_general | solution.py:141
  46.5 3.3 %convolution_bitcast_fusion = f32[27,96,96]{1,2,0:T(8,128)} fusion(f32[27,27,96]{2,1,0:T(8,128)S(1)} %convolution_bitcast_fusion.6, f32[96,27,1]{0,1,2:T(8,128)S(1)} %copy-done.13), kind=kOutput, calls=%fused_computation.37 | convolution fusion | flops 80621568 | bytes 1285632 | tf_op jit(solution)/shard_map/while/body/eval_jaxpr/bj,ijc->ibc/dot_general | solution.py:147
  49.8 2.8 %copy.46 = f32[27,96,96]{2,1,0:T(8,128)} copy(f32[27,96,96]{1,2,0:T(8,128)} %convolution_bitcast_fusion) | data formatting | bytes 1990656 | tf_op jit(solution)/shard_map/while/body/eval_jaxpr/bj,ijc->ibc/transpose | solution.py:147
  52.6 3.2 %reshape.442 = f32[27,9216]{1,0:T(8,128)} reshape(f32[27,96,96]{2,1,0:T(8,128)} %copy.46) | data formatting | bytes 1990656 | tf_op jit(solution)/shard_map/while/body/eval_jaxpr/reshape | solution.py:147
  55.8 1.5 copy.45
  57.3 3.2 %reshape.440 = f32[27,9216]{1,0:T(8,128)} reshape(f32[27,96,96]{2,1,0:T(8,128)} %copy.45) | data formatting | bytes 1990656 | tf_op jit(solution)/shard_map/while/body/eval_jaxpr/reshape | solution.py:144
  60.9 1.9 %reshape.436 = f32[27,9216]{1,0:T(8,128)} reshape(f32[27,96,96]{2,1,0:T(8,128)S(1)} %copy.42) | data formatting | bytes 1990656 | tf_op jit(solution)/shard_map/while/body/eval_jaxpr/reshape | solution.py:141
  62.8 4.7 %fusion.68 = f32[96,9216]{1,0:T(8,128)S(1)} fusion(f32[96,27]{0,1:T(8,128)S(1)} %copy-done.15, f32[27,9216]{1,0:T(8,128)} %reshape.440), kind=kOutput, calls=%fused_computation.118 | convolution fusion | flops 286654464 | bytes 4544640 | tf_op jit(solution)/shard_map/while/body/eval_jaxpr/dot_general | solution.py:152
  67.5 3.0 %fusion.70 = f32[96,9216]{1,0:T(8,128)S(1)} fusion(f32[96,27]{0,1:T(8,128)S(1)} %copy-done.15, f32[27,9216]{1,0:T(8,128)S(1)} %copy-done.6), kind=kOutput, calls=%fused_computation.120 | convolution fusion | flops 286654464 | bytes 4544640 | tf_op jit(solution)/shard_map/while/body/eval_jaxpr/dot_general | solution.py:153
  70.5 3.0 %fusion.64 = f32[96,9216]{1,0:T(8,128)S(1)} fusion(f32[96,27]{0,1:T(8,128)S(1)} %copy-done.20, f32[27,9216]{1,0:T(8,128)S(1)} %copy-done.7), kind=kOutput, calls=%fused_computation.114 | convolution fusion | flops 286654464 | bytes 4544640 | tf_op jit(solution)/shard_map/while/body/eval_jaxpr/dot_general | solution.py:151
  73.5 1.8 copy-done.3
  75.3 4.4 %fusion.13 = f32[27,9216]{1,0:T(8,128)S(1)} fusion(f32[96,27]{0,1:T(8,128)S(1)} %copy-done.16, f32[1,96,9216]{2,1,0:T(8,128)S(1)} %copy-done, f32[96,9216]{1,0:T(8,128)S(1)} %fusion.70, f32[96,9216]{1,0:T(8,128)S(1)} %fusion.68, f32[96,9216]{1,0:T(8,128)S(1)} %fusion.64, f32[]{:T(128)} %bitcast.17, f32[]{:T(128)} %bitcast.12, f32[]{:T(128)} %bitcast.4), kind=kOutput, calls=%fused_computation.14 | convolution fusion | flops 291962880 | bytes 15161484 | tf_op jit(solution)/shard_map/while/body/eval_jaxpr/dot_general | solution.py:127
  80.3 0.9 convolution_bitcast_fusion.4
  81.2 0.7 convolution_negate_fusion
  81.9 0.9 neg.15
  84.2 0.7 fusion.58
  87.6 0.7 eq.41
  88.6 0.7 reshape.455
  89.5 0.7 and.41
  90.2 0.7 stack_reshape.2
  92.2 9.6 %all-gather = f32[4,7,729]{2,1,0:T(8,128)S(1)} all-gather(f32[1,7,729]{2,1,0:T(8,128)S(1)} %dynamic-slice_bitcast_fusion), channel_id=1, replica_groups=mesh['patch'=64,'sub'=4] {'sub'}, dimensions={0}, use_global_device_ids=true | all-gather | bytes 102060 | tf_op jit(solution)/shard_map/all_gather | solution.py:46
  102.7 2.2 %convolution_bitcast_fusion.2 = f32[27,96,96]{1,2,0:T(8,128)S(1)} fusion(f32[27,27,96]{2,1,0:T(8,128)S(1)} %fusion.65, f32[96,27,1]{0,1,2:T(8,128)S(1)} %copy-done.13), kind=kOutput, calls=%fused_computation.39 | convolution fusion | flops 80621568 | bytes 1285632 | tf_op jit(solution)/shard_map/while/body/eval_jaxpr/bj,ijc->ibc/dot_general | solution.py:115
  105.4 1.9 %reshape.438 = f32[27,9216]{1,0:T(8,128)} reshape(f32[27,96,96]{2,1,0:T(8,128)S(1)} %copy.44) | data formatting | bytes 1990656 | tf_op jit(solution)/shard_map/while/body/eval_jaxpr/reshape | solution.py:118
  107.3 4.4 %fusion.66 = f32[96,9216]{1,0:T(8,128)S(1)} fusion(f32[96,27]{0,1:T(8,128)} %constant.177.clone, f32[27,9216]{1,0:T(8,128)} %reshape.438), kind=kOutput, calls=%fused_computation.116 | convolution fusion | flops 286654464 | bytes 4544640 | tf_op jit(solution)/shard_map/while/body/eval_jaxpr/dot_general | solution.py:116
  111.7 7.2 %fusion.7 = f32[27,9216]{1,0:T(8,128)} fusion(f32[96,27]{0,1:T(8,128)S(1)} %copy-done.17, f32[96,9216]{1,0:T(8,128)S(1)} %fusion.66, f32[1,96,9216]{2,1,0:T(8,128)S(1)} %copy-done.1, f32[96,9216]{1,0:T(8,128)} %copy-done.4, f32[1,96,9216]{2,1,0:T(8,128)} %param.20, f32[]{:T(128)} %bitcast.12, f32[]{:T(128)S(6)} %select_n.60), kind=kOutput, calls=%fused_computation.10 | convolution fusion | flops 291078144 | bytes 15161480 | tf_op jit(solution)/shard_map/while/body/eval_jaxpr/dot_general | solution.py:163
  118.9 2.0 %stack.14 = f32[64,8,1,729]{3,1,2,0:T(8,128)} broadcast(f32[8,729]{1,0:T(8,128)} %stack_reshape.2), dimensions={1,3} | broadcast | bytes 1516320 | tf_op jit(solution)/shard_map/stack | solution.py:28
  120.9 13.2 %all-to-all-start = ((f32[64,8,1,729]{3,1,2,0:T(8,128)}), f32[64,8,1,729]{3,1,2,0:T(8,128)}, u32[]{:S(2)}, u32[]{:S(2)}) async-start(f32[64,8,1,729]{3,1,2,0:T(8,128)} %stack.14), calls=%async_computation | async-start | bytes 3145728 | tf_op jit(solution)/shard_map/all_to_all | solution.py:29
  134.2 8.3 %fusion.3 = f32[27,9216]{1,0:T(8,128)} fusion(f32[96,27]{0,1:T(8,128)} %constant.180.clone, f32[96,9216]{1,0:T(8,128)S(1)} %fusion.66, f32[1,96,9216]{2,1,0:T(8,128)} %param.21, f32[96,9216]{1,0:T(8,128)} %copy-done.3, f32[1,96,9216]{2,1,0:T(8,128)} %param.20, f32[]{:T(128)} %bitcast.4, f32[]{:T(128)S(6)} %select_n.60), kind=kOutput, calls=%fused_computation.7 | convolution fusion | flops 291078144 | bytes 15161480 | tf_op jit(solution)/shard_map/while/body/eval_jaxpr/dot_general | solution.py:160
  142.4 2.9 %reshape.439 = f32[27,96,96]{2,1,0:T(8,128)} reshape(f32[27,9216]{1,0:T(8,128)} %fusion.3) | data formatting | bytes 1990656 | tf_op jit(solution)/shard_map/while/body/eval_jaxpr/reshape | solution.py:160
  145.3 2.9 %reshape.441 = f32[27,96,96]{2,1,0:T(8,128)} reshape(f32[27,9216]{1,0:T(8,128)} %fusion.7) | data formatting | bytes 1990656 | tf_op jit(solution)/shard_map/while/body/eval_jaxpr/reshape | solution.py:163
  148.2 8.2 %fusion.11 = f32[27,9216]{1,0:T(8,128)} fusion(f32[96,27]{0,1:T(8,128)} %constant.179.clone, f32[96,9216]{1,0:T(8,128)S(1)} %fusion.66, f32[1,96,9216]{2,1,0:T(8,128)} %param.21, f32[96,9216]{1,0:T(8,128)} %copy-done.2, f32[1,96,9216]{2,1,0:T(8,128)} %param.20, f32[]{:T(128)} %bitcast.17, f32[]{:T(128)S(6)} %select_n.60), kind=kOutput, calls=%fused_computation.13 | convolution fusion | flops 291078144 | bytes 15161480 | tf_op jit(solution)/shard_map/while/body/eval_jaxpr/dot_general | solution.py:166
  156.3 1.9 %reshape.443 = f32[27,96,96]{2,1,0:T(8,128)S(1)} reshape(f32[27,9216]{1,0:T(8,128)} %fusion.11) | data formatting | bytes 1990656 | tf_op jit(solution)/shard_map/while/body/eval_jaxpr/reshape | solution.py:166
  158.2 2.2 %fusion.67 = f32[27,96,27]{1,2,0:T(8,128)S(1)} fusion(f32[27,96,96]{2,1,0:T(8,128)} %reshape.439, f32[96,27,1]{0,1,2:T(8,128)S(1)} %copy-done.12), kind=kOutput, calls=%fused_computation.117 | convolution fusion | flops 80621568 | bytes 1285632 | tf_op jit(solution)/shard_map/while/body/eval_jaxpr/bj,ibc->ijc/dot_general | solution.py:169
  160.5 0.9 fusion.33
  161.9 0.9 convolution_bitcast_fusion.5
  164.0 1.4 reshape.456
  165.4 0.7 gather_fusion
  167.0 0.7 sub.32
  167.7 5.9 %all-to-all-done = f32[64,8,1,729]{3,1,2,0:T(8,128)} async-done(((f32[64,8,1,729]{3,1,2,0:T(8,128)}), f32[64,8,1,729]{3,1,2,0:T(8,128)}, u32[]{:S(2)}, u32[]{:S(2)}) %all-to-all-start) | async-done | bytes 1493024 | tf_op jit(solution)/shard_map/all_to_all | solution.py:29
  173.7 2.0 %fusion.31 = f32[4,729]{1,0:T(4,128)S(1)} fusion(f32[64,8,1,729]{3,1,2,0:T(8,128)} %all-to-all-done, s32[512]{0:T(512)S(1)} %copy-done.23, pred[512]{0:T(512)(128)(4,1)S(1)} %copy-done.25), kind=kOutput, calls=%fused_computation.35 | convolution fusion | flops 17920000 | bytes 1507216 | tf_op jit(solution)/shard_map/ft,tvx->fvx/dot_general | solution.py:255
  176.4 1.0 reshape.452
  (135 shorter events, 14.1 us)
Async XLA Ops:
  7.2 33.2 %copy-start.13 = (f32[96,27,1]{0,1,2:T(8,128)S(1)}, f32[96,27,1]{0,1,2:T(8,128)}, u32[]{:S(2)}) copy-start(f32[96,27,1]{0,1,2:T(8,128)} %constant.193) | copy-start | bytes 31108
  7.2 33.7 %copy-start.19 = (f32[96,27,1]{0,1,2:T(8,128)S(1)}, f32[96,27,1]{0,1,2:T(8,128)}, u32[]{:S(2)}) copy-start(f32[96,27,1]{0,1,2:T(8,128)} %constant.195) | copy-start | bytes 31108
  18.7 73.4 %collective-permute-start = (f32[3,729]{1,0:T(4,128)S(1)}, f32[3,729]{1,0:T(4,128)S(1)}, u32[]{:S(2)}, u32[]{:S(2)}) collective-permute-start(f32[3,729]{1,0:T(4,128)S(1)} %slice.223), channel_id=1, source_target_pairs={{0,1},{1,2},{2,3},{4,5},{5,6},{6,7},{8,9},{9,10},{10,11},{12,13},{... | collective-permute-start | bytes 26252
  24.5 94.4 %all-to-all-start.1 = ((f32[64,1,4,1,729]{4,2,3,1,0:T(4,128)}), f32[64,1,4,1,729]{4,2,3,1,0:T(4,128)}, u32[]{:S(2)}, u32[]{:S(2)}) async-start(f32[64,1,4,1,729]{4,2,3,1,0:T(4,128)} %broadcast_in_dim.45), calls=%async_computation.1 | async-start | bytes 1572864 | tf_op jit(solution)/shard_map/all_to_all | solution.py:57
  39.7 123.9 %all-reduce.5.cloned.1.call-start = ((), (), s32[]{:S(2)}) async-start(), calls=%async_computation.2 | async-start | bytes 196608 | tf_op jit(solution)/shard_map/psum | solution.py:213
  57.3 5.5 %copy-start.15 = (f32[96,27]{0,1:T(8,128)S(1)}, f32[96,27]{0,1:T(8,128)}, u32[]{:S(2)}) copy-start(f32[96,27]{0,1:T(8,128)} %constant.177.clone) | copy-start | bytes 31108
  60.9 6.5 %copy-start.6 = (f32[27,9216]{1,0:T(8,128)S(1)}, f32[27,9216]{1,0:T(8,128)}, u32[]{:S(2)}) copy-start(f32[27,9216]{1,0:T(8,128)} %reshape.442) | copy-start | bytes 2985988
  67.5 6.0 %copy-start.4 = (f32[96,9216]{1,0:T(8,128)}, f32[96,9216]{1,0:T(8,128)S(1)}, u32[]{:S(2)}) copy-start(f32[96,9216]{1,0:T(8,128)S(1)} %fusion.68) | copy-start | bytes 10616836
  67.5 3.0 %copy-start.7 = (f32[27,9216]{1,0:T(8,128)S(1)}, f32[27,9216]{1,0:T(8,128)}, u32[]{:S(2)}) copy-start(f32[27,9216]{1,0:T(8,128)} %reshape.436) | copy-start | bytes 2985988
  67.5 3.0 %copy-start.20 = (f32[96,27]{0,1:T(8,128)S(1)}, f32[96,27]{0,1:T(8,128)}, u32[]{:S(2)}) copy-start(f32[96,27]{0,1:T(8,128)} %constant.178.clone) | copy-start | bytes 31108
  70.5 3.0 %copy-start.2 = (f32[96,9216]{1,0:T(8,128)}, f32[96,9216]{1,0:T(8,128)S(1)}, u32[]{:S(2)}) copy-start(f32[96,9216]{1,0:T(8,128)S(1)} %fusion.70) | copy-start | bytes 10616836
  70.5 4.8 %copy-start = (f32[1,96,9216]{2,1,0:T(8,128)S(1)}, f32[1,96,9216]{2,1,0:T(8,128)}, u32[]{:S(2)}) copy-start(f32[1,96,9216]{2,1,0:T(8,128)} %param.21) | copy-start | bytes 10616836
  70.5 4.8 %copy-start.16 = (f32[96,27]{0,1:T(8,128)S(1)}, f32[96,27]{0,1:T(8,128)}, u32[]{:S(2)}) copy-start(f32[96,27]{0,1:T(8,128)} %constant.179.clone) | copy-start | bytes 31108
  73.5 1.8 copy-start.3
  75.3 5.0 %copy-start.12 = (f32[96,27,1]{0,1,2:T(8,128)S(1)}, f32[96,27,1]{0,1,2:T(8,128)}, u32[]{:S(2)}) copy-start(f32[96,27,1]{0,1,2:T(8,128)} %constant.194) | copy-start | bytes 31108
  79.7 3.0 %copy-start.21 = (s32[256,6]{0,1:T(8,128)S(1)}, s32[256,6]{0,1:T(8,128)}, u32[]{:S(2)}) copy-start(s32[256,6]{0,1:T(8,128)} %param.24) | copy-start | bytes 18436
  79.7 3.3 %copy-start.22 = (f32[4,1,1,729]{3,2,1,0:T(1,128)S(1)}, f32[4,1,1,729]{3,2,1,0:T(1,128)}, u32[]{:S(2)}) copy-start(f32[4,1,1,729]{3,2,1,0:T(1,128)} %param.22) | copy-start | bytes 34996
  79.8 5.8 %copy-start.14 = (f32[4,2,2,27,27]{4,2,3,1,0:T(2,128)S(1)}, f32[4,2,2,27,27]{4,2,3,1,0:T(2,128)}, u32[]{:S(2)}) copy-start(f32[4,2,2,27,27]{4,2,3,1,0:T(2,128)} %param.23) | copy-start | bytes 139972
  79.8 6.9 %copy-start.27 = (f32[2]{0:T(128)S(1)}, f32[2]{0:T(128)}, u32[]{:S(2)}) copy-start(f32[2]{0:T(128)} %constant.181.clone) | copy-start | bytes 28
  80.3 10.6 %copy-start.28 = (u32[256]{0:T(256)S(1)}, u32[256]{0:T(256)}, u32[]{:S(2)}) copy-start(u32[256]{0:T(256)} %constant.191) | copy-start | bytes 3076
  86.0 0.6 copy-start.8
  86.0 0.9 copy-start.10
  107.3 4.4 %copy-start.1 = (f32[1,96,9216]{2,1,0:T(8,128)S(1)}, f32[1,96,9216]{2,1,0:T(8,128)}, u32[]{:S(2)}) copy-start(f32[1,96,9216]{2,1,0:T(8,128)} %param.21) | copy-start | bytes 10616836
  107.3 4.4 %copy-start.17 = (f32[96,27]{0,1:T(8,128)S(1)}, f32[96,27]{0,1:T(8,128)}, u32[]{:S(2)}) copy-start(f32[96,27]{0,1:T(8,128)} %constant.179.clone) | copy-start | bytes 31108
  120.9 52.7 %all-to-all-start = ((f32[64,8,1,729]{3,1,2,0:T(8,128)}), f32[64,8,1,729]{3,1,2,0:T(8,128)}, u32[]{:S(2)}, u32[]{:S(2)}) async-start(f32[64,8,1,729]{3,1,2,0:T(8,128)} %stack.14), calls=%async_computation | async-start | bytes 3145728 | tf_op jit(solution)/shard_map/all_to_all | solution.py:29
  156.3 4.1 %copy-start.5 = (f32[27,96,96]{2,1,0:T(8,128)S(1)}, f32[27,96,96]{2,1,0:T(8,128)}, u32[]{:S(2)}) copy-start(f32[27,96,96]{2,1,0:T(8,128)} %reshape.441) | copy-start | bytes 2985988
  156.3 4.1 %copy-start.18 = (f32[96,27,1]{0,1,2:T(8,128)S(1)}, f32[96,27,1]{0,1,2:T(8,128)}, u32[]{:S(2)}) copy-start(f32[96,27,1]{0,1,2:T(8,128)} %constant.196) | copy-start | bytes 31108
  161.3 4.9 %copy-start.11 = (f32[4,2,27,27]{3,1,2,0:T(2,128)S(1)}, f32[4,2,27,27]{3,1,2,0:T(2,128)}, u32[]{:S(2)}) copy-start(f32[4,2,27,27]{3,1,2,0:T(2,128)} %copy-done.10) | copy-start | bytes 69988
  161.3 4.9 %copy-start.24 = (f32[4,2]{1,0:T(4,128)S(1)}, f32[4,2]{1,0:T(4,128)}, u32[]{:S(2)}) copy-start(f32[4,2]{1,0:T(4,128)} %reshape.455) | copy-start | bytes 100
  161.4 4.9 %copy-start.26 = (pred[4,2]{1,0:T(4,128)(4,1)S(1)}, pred[4,2]{1,0:T(4,128)(4,1)}, u32[]{:S(2)}) copy-start(pred[4,2]{1,0:T(4,128)(4,1)} %compare_and_fusion.1) | copy-start | bytes 28
  161.9 4.8 %copy-start.9 = (f32[4,2,27,27]{3,1,2,0:T(2,128)S(1)}, f32[4,2,27,27]{3,1,2,0:T(2,128)}, u32[]{:S(2)}) copy-start(f32[4,2,27,27]{3,1,2,0:T(2,128)} %copy-done.8) | copy-start | bytes 69988
  161.9 11.8 %copy-start.23 = (s32[512]{0:T(512)S(1)}, s32[512]{0:T(512)}, u32[]{:S(2)}) copy-start(s32[512]{0:T(512)} %eq.41) | copy-start | bytes 6148
  161.9 11.8 %copy-start.25 = (pred[512]{0:T(512)(128)(4,1)S(1)}, pred[512]{0:T(512)(128)(4,1)}, u32[]{:S(2)}) copy-start(pred[512]{0:T(512)(128)(4,1)} %and.41) | copy-start | bytes 1540
Sparse Core Ops, SparseCore 0:
  82.9 43.8 all-reduce.4
